TPU v7x, 32 devices: a whole 2x2x4 slice. The times are simulated.
32 devices in a mesh: groups: 2 (over y), pages: 4 (over z), patches: 4 (over x, core).
Axes of the slice: x: 2, y: 2, z: 4, core: 2. Of those that a mesh axis runs over, the one named last changes fastest.
Arguments:
- queries: bfloat16 [16, 32, 128], P(('groups', 'pages'), 'patches'), parts along dimension 0, may hold values from -6 to 6
- gallery: bfloat16 [640, 1024, 128], P(('groups', 'pages'), 'patches'), parts along dimension 0, may hold values from -0.5 to 0.5
- page_rows: int32 [640], P('groups'), parts along dimension 0, may hold values from 0 to 319, as said below
- candidates: int32 [16, 32], P(('groups', 'pages')), parts along dimension 0, may hold values from 0 to 319, as said below
Outputs:
- scores: float32 [16, 32], P(('groups', 'pages')), parts along dimension 0
There are 2 independent parts, one for each index of `groups`. A program takes and returns all parts, laid end to end along the dimension named above; each array names one. Nothing has to cross between parts.
Inputs may be any that keep to these rules, and one draw needn't show every extreme that they name: A permutation: page id c is stored at row page_rows[c] of gallery, which lies on pages index page_rows[c] // 80. Each query's 32 page ids are distinct. The 2 queries of one pages index have at most 48 candidates stored on one pages index, and in every draw some pages index stores exactly 48 candidates of the queries of every pages index.
All inputs are finite; a program needn't handle non-finite values.
Results may differ from a plain program's by a relative error of at most 0.0003.
Values may be sent and summed in bfloat16 or wider, within the bound.
A program may use at most 64 MiB of HBM per device.

v0:
```python
import jax
import jax.numpy as jnp
from jax import lax
from jax.sharding import PartitionSpec as P

QT = 32
CAP = 48


def token_maxima(query_rows, gallery):
    page_count = gallery.shape[0]
    grouped = gallery.reshape(page_count // 8, 8, gallery.shape[1], gallery.shape[2])

    def per_block(block):
        sims = jnp.einsum("rd,bpd->brp", query_rows, block, preferred_element_type=jnp.float32)
        return jnp.max(sims, axis=2)

    result = lax.map(per_block, grouped)
    return result.reshape(page_count, query_rows.shape[0])


def slot_plan(storage, page_count, owner_count, query_count):
    flat_rows = storage.reshape(-1)
    holder = flat_rows // page_count
    local_page = flat_rows % page_count
    onehot = (holder[:, None] == jnp.arange(owner_count, dtype=jnp.int32)[None, :]).astype(
        jnp.int32
    )
    running = jnp.cumsum(onehot, axis=0) - onehot
    rank = jnp.sum(running * onehot, axis=1)
    query_ids = (
        lax.axis_index("pages") * query_count + jnp.arange(query_count, dtype=jnp.int32)[:, None]
    )
    query_ids = jnp.broadcast_to(query_ids, storage.shape).reshape(-1)
    codes = (
        jnp.full((owner_count, CAP), -1, jnp.int32)
        .at[holder, rank]
        .set(query_ids * page_count + local_page)
    )
    return (holder, rank, codes)


def body(queries, gallery, page_rows, candidates):
    query_count = queries.shape[0]
    page_count = gallery.shape[0]
    owner_count = lax.axis_size("pages")
    storage = jnp.take(page_rows, candidates, axis=0)
    local_tokens = lax.all_gather(queries, "patches", axis=1, tiled=True)
    shard_rows = lax.all_gather(local_tokens, "pages", axis=0, tiled=True)
    maxima = token_maxima(shard_rows.reshape(-1, shard_rows.shape[2]), gallery)
    part_count = lax.axis_size("patches")
    arrived = lax.all_to_all(maxima, "patches", split_axis=0, concat_axis=0, tiled=True)
    share_max = jnp.max(arrived.reshape(part_count, page_count // part_count, -1), axis=0)
    share_scores = jnp.mean(share_max.reshape(page_count // part_count, -1, QT), axis=2)
    page_scores = lax.all_gather(share_scores, "patches", axis=0, tiled=True)
    holder, rank, codes = slot_plan(storage, page_count, owner_count, query_count)
    incoming = lax.all_to_all(codes, "pages", split_axis=0, concat_axis=0, tiled=True)
    safe_codes = jnp.maximum(incoming, 0)
    picked = page_scores[safe_codes % page_count, safe_codes // page_count]
    picked = jnp.where(incoming >= 0, picked, 0.0)
    returned = lax.all_to_all(picked, "pages", split_axis=0, concat_axis=0, tiled=True)
    return returned[holder, rank].reshape(storage.shape)


def solution(mesh):
    in_specs = (
        P(("groups", "pages"), "patches", None),
        P(("groups", "pages"), "patches", None),
        P("groups"),
        P(("groups", "pages"), None),
    )
    out_specs = P(("groups", "pages"), None)
    return jax.shard_map(body, mesh=mesh, in_specs=in_specs, out_specs=out_specs, check_vma=False)
```

profile of v0, /device:TPU:0, one launch (start us, length us, event | category | flops | bytes accessed | tf_op | source)
XLA Modules:
  0.0 81.3 jit_solution(7018582230763072979)
XLA Ops:
  0.0 0.7 compare_select_fusion.3
  0.8 0.8 gather_fusion
  1.7 0.7 compare_and_fusion
  3.9 10.2 %scatter_fusion = s32[4,48]{1,0:T(4,128)} fusion(s32[4,48]{1,0:T(4,128)} %broadcast_in_dim.36, s32[64]{0:T(128)S(1)} %get-tuple-element.42, s32[64]{0:T(128)S(1)} %get-tuple-element.45), kind=kCustom, calls=%fused_computation.3 | custom fusion | bytes 1280 | tf_op jit(solution)/shard_map/scatter | solution.py:38
  14.1 6.3 %all-to-all-start = ((s32[4,1,48]{2,1,0:T(1,128)}), s32[4,1,48]{2,1,0:T(1,128)S(1)}, u32[]{:S(2)}, u32[]{:S(2)}) async-start(s32[4,1,48]{2,1,0:T(1,128)} %bitcast.6), calls=%async_computation | async-start | bytes 4096 | tf_op jit(solution)/shard_map/all_to_all | solution.py:57
  20.5 5.4 %all_gather.9 = bf16[2,32,128]{2,1,0:T(8,128)(2,1)S(1)} all-gather(bf16[2,8,128]{2,1,0:T(8,128)(2,1)} %param.6), channel_id=1, replica_groups=mesh['groups'=2,'pages'=4,'patches'=4] {'patches'}, dimensions={1}, use_global_device_ids=true | all-gather | bytes 20480 | tf_op jit(solution)/shard_map/all_gather | solution.py:48
  25.9 13.7 %all_gather.10 = bf16[8,32,128]{2,1,0:T(8,128)(2,1)S(1)} all-gather(bf16[2,32,128]{2,1,0:T(8,128)(2,1)S(1)} %all_gather.9), channel_id=1, replica_groups=mesh['groups'=2,'pages'=4,'patches'=4] {'pages'}, dimensions={0}, use_global_device_ids=true | all-gather | bytes 81920 | tf_op jit(solution)/shard_map/all_gather | solution.py:49
  39.5 15.2 %while.10 = (s32[]{:T(128)}, f32[10,8,256]{2,1,0:T(8,128)S(1)}, bf16[10,8,256,128]{3,2,1,0:T(8,128)(2,1)}, bf16[256,128]{1,0:T(8,128)(2,1)S(1)}, s32[]{:T(128)}) while((s32[]{:T(128)}, f32[10,8,256]{2,1,0:T(8,128)S(1)}, bf16[10,8,256,128]{3,2,1,0:T(8,128)(2,1)}, bf16[256,128]{1,0:T(8,128)(2,1)S(1)}, s32[]{:T(128)}) %tuple.28), condition=%wide.region_5.6_spmd, body=%wide.region_3.5_spmd.sunk | while | flops 134739968 | bytes 614477 | solution.py:18
  39.5 1.5 %convolution_reduce_fusion.2 = f32[8,256]{1,0:T(8,128)S(1)} fusion(bf16[10,8,256,128]{3,2,1,0:T(8,128)(2,1)} %get-tuple-element.84, s32[]{:T(128)S(6)} %copy.20, bf16[256,128]{1,0:T(8,128)(2,1)S(1)} %get-tuple-element.85), kind=kOutput, calls=%fused_computation.4.clone.1 | convolution fusion | flops 134739968 | bytes 598020 | tf_op jit(solution)/shard_map/while/body/eval_jaxpr/rd,bpd->brp/dot_general | solution.py:15
  41.1 1.5 %convolution_reduce_fusion.2 = f32[8,256]{1,0:T(8,128)S(1)} fusion(bf16[10,8,256,128]{3,2,1,0:T(8,128)(2,1)} %get-tuple-element.84, s32[]{:T(128)S(6)} %copy.20, bf16[256,128]{1,0:T(8,128)(2,1)S(1)} %get-tuple-element.85), kind=kOutput, calls=%fused_computation.4.clone.1 | convolution fusion | flops 134739968 | bytes 598020 | tf_op jit(solution)/shard_map/while/body/eval_jaxpr/rd,bpd->brp/dot_general | solution.py:15
  42.6 1.5 %convolution_reduce_fusion.2 = f32[8,256]{1,0:T(8,128)S(1)} fusion(bf16[10,8,256,128]{3,2,1,0:T(8,128)(2,1)} %get-tuple-element.84, s32[]{:T(128)S(6)} %copy.20, bf16[256,128]{1,0:T(8,128)(2,1)S(1)} %get-tuple-element.85), kind=kOutput, calls=%fused_computation.4.clone.1 | convolution fusion | flops 134739968 | bytes 598020 | tf_op jit(solution)/shard_map/while/body/eval_jaxpr/rd,bpd->brp/dot_general | solution.py:15
  44.1 1.5 %convolution_reduce_fusion.2 = f32[8,256]{1,0:T(8,128)S(1)} fusion(bf16[10,8,256,128]{3,2,1,0:T(8,128)(2,1)} %get-tuple-element.84, s32[]{:T(128)S(6)} %copy.20, bf16[256,128]{1,0:T(8,128)(2,1)S(1)} %get-tuple-element.85), kind=kOutput, calls=%fused_computation.4.clone.1 | convolution fusion | flops 134739968 | bytes 598020 | tf_op jit(solution)/shard_map/while/body/eval_jaxpr/rd,bpd->brp/dot_general | solution.py:15
  45.6 1.5 %convolution_reduce_fusion.2 = f32[8,256]{1,0:T(8,128)S(1)} fusion(bf16[10,8,256,128]{3,2,1,0:T(8,128)(2,1)} %get-tuple-element.84, s32[]{:T(128)S(6)} %copy.20, bf16[256,128]{1,0:T(8,128)(2,1)S(1)} %get-tuple-element.85), kind=kOutput, calls=%fused_computation.4.clone.1 | convolution fusion | flops 134739968 | bytes 598020 | tf_op jit(solution)/shard_map/while/body/eval_jaxpr/rd,bpd->brp/dot_general | solution.py:15
  47.2 1.5 %convolution_reduce_fusion.2 = f32[8,256]{1,0:T(8,128)S(1)} fusion(bf16[10,8,256,128]{3,2,1,0:T(8,128)(2,1)} %get-tuple-element.84, s32[]{:T(128)S(6)} %copy.20, bf16[256,128]{1,0:T(8,128)(2,1)S(1)} %get-tuple-element.85), kind=kOutput, calls=%fused_computation.4.clone.1 | convolution fusion | flops 134739968 | bytes 598020 | tf_op jit(solution)/shard_map/while/body/eval_jaxpr/rd,bpd->brp/dot_general | solution.py:15
  48.7 1.5 %convolution_reduce_fusion.2 = f32[8,256]{1,0:T(8,128)S(1)} fusion(bf16[10,8,256,128]{3,2,1,0:T(8,128)(2,1)} %get-tuple-element.84, s32[]{:T(128)S(6)} %copy.20, bf16[256,128]{1,0:T(8,128)(2,1)S(1)} %get-tuple-element.85), kind=kOutput, calls=%fused_computation.4.clone.1 | convolution fusion | flops 134739968 | bytes 598020 | tf_op jit(solution)/shard_map/while/body/eval_jaxpr/rd,bpd->brp/dot_general | solution.py:15
  50.2 1.5 %convolution_reduce_fusion.2 = f32[8,256]{1,0:T(8,128)S(1)} fusion(bf16[10,8,256,128]{3,2,1,0:T(8,128)(2,1)} %get-tuple-element.84, s32[]{:T(128)S(6)} %copy.20, bf16[256,128]{1,0:T(8,128)(2,1)S(1)} %get-tuple-element.85), kind=kOutput, calls=%fused_computation.4.clone.1 | convolution fusion | flops 134739968 | bytes 598020 | tf_op jit(solution)/shard_map/while/body/eval_jaxpr/rd,bpd->brp/dot_general | solution.py:15
  51.7 1.5 %convolution_reduce_fusion.2 = f32[8,256]{1,0:T(8,128)S(1)} fusion(bf16[10,8,256,128]{3,2,1,0:T(8,128)(2,1)} %get-tuple-element.84, s32[]{:T(128)S(6)} %copy.20, bf16[256,128]{1,0:T(8,128)(2,1)S(1)} %get-tuple-element.85), kind=kOutput, calls=%fused_computation.4.clone.1 | convolution fusion | flops 134739968 | bytes 598020 | tf_op jit(solution)/shard_map/while/body/eval_jaxpr/rd,bpd->brp/dot_general | solution.py:15
  53.3 1.5 %convolution_reduce_fusion.2 = f32[8,256]{1,0:T(8,128)S(1)} fusion(bf16[10,8,256,128]{3,2,1,0:T(8,128)(2,1)} %get-tuple-element.84, s32[]{:T(128)S(6)} %copy.20, bf16[256,128]{1,0:T(8,128)(2,1)S(1)} %get-tuple-element.85), kind=kOutput, calls=%fused_computation.4.clone.1 | convolution fusion | flops 134739968 | bytes 598020 | tf_op jit(solution)/shard_map/while/body/eval_jaxpr/rd,bpd->brp/dot_general | solution.py:15
  55.4 3.3 %all-to-all-start.1 = ((f32[4,20,256]{2,1,0:T(8,128)}), f32[4,20,256]{2,1,0:T(8,128)S(1)}, u32[]{:S(2)}, u32[]{:S(2)}) async-start(f32[4,20,256]{2,1,0:T(8,128)} %all_to_all.20), calls=%async_computation.1 | async-start | bytes 196608 | tf_op jit(solution)/shard_map/all_to_all | solution.py:52
  59.1 3.9 %all-to-all-done.1 = f32[4,20,256]{2,1,0:T(8,128)S(1)} async-done(((f32[4,20,256]{2,1,0:T(8,128)}), f32[4,20,256]{2,1,0:T(8,128)S(1)}, u32[]{:S(2)}, u32[]{:S(2)}) %all-to-all-start.1) | async-done | bytes 81952 | tf_op jit(solution)/shard_map/all_to_all | solution.py:52
  63.3 5.2 %all-gather = f32[4,20,8]{1,2,0:T(8,128)S(1)} all-gather(f32[1,20,8]{1,2,0:T(8,128)S(1)} %copy.12), channel_id=1, replica_groups=mesh['groups'=2,'pages'=4,'patches'=4] {'patches'}, dimensions={0}, use_global_device_ids=true | all-gather | bytes 3200 | tf_op jit(solution)/shard_map/all_gather | solution.py:55
  68.6 1.2 %gather_fusion.1 = f32[192]{0:T(256)S(1)} fusion(f32[80,8]{0,1:T(8,128)S(1)} %reshape.242, s32[192]{0:T(256)S(1)} %reshape.220), kind=kCustom, calls=%fused_computation.1 | custom fusion | bytes 3072 | tf_op jit(solution)/shard_map/gather | solution.py:59
  69.8 9.9 %all_to_all.27 = f32[4,1,48]{2,1,0:T(1,128)S(1)} all-to-all(f32[4,1,48]{2,1,0:T(1,128)S(1)} %compare_select_fusion), channel_id=1, replica_groups=mesh['groups'=2,'pages'=4,'patches'=4] {'pages'}, dimensions={0} | all-to-all | bytes 1536 | tf_op jit(solution)/shard_map/all_to_all | solution.py:61
  79.7 0.9 %gather_fusion.2 = f32[64]{0:T(128)S(1)} fusion(f32[4,48]{1,0:T(4,128)S(1)} %bitcast.60, s32[64]{0:T(128)S(1)} %get-tuple-element.41), kind=kCustom, calls=%fused_computation.2 | custom fusion | bytes 1024 | tf_op jit(solution)/shard_map/gather | solution.py:62
  (47 shorter events, 3.9 us)
Async XLA Ops:
  0.0 0.8 copy-start
  14.1 41.3 %all-to-all-start = ((s32[4,1,48]{2,1,0:T(1,128)}), s32[4,1,48]{2,1,0:T(1,128)S(1)}, u32[]{:S(2)}, u32[]{:S(2)}) async-start(s32[4,1,48]{2,1,0:T(1,128)} %bitcast.6), calls=%async_computation | async-start | bytes 4096 | tf_op jit(solution)/shard_map/all_to_all | solution.py:57
  55.4 7.6 %all-to-all-start.1 = ((f32[4,20,256]{2,1,0:T(8,128)}), f32[4,20,256]{2,1,0:T(8,128)S(1)}, u32[]{:S(2)}, u32[]{:S(2)}) async-start(f32[4,20,256]{2,1,0:T(8,128)} %all_to_all.20), calls=%async_computation.1 | async-start | bytes 196608 | tf_op jit(solution)/shard_map/all_to_all | solution.py:52
where the time goes:
time: 82.3 us; the launch traced here: 81.3 us
  blocking collectives  34.2 us (42%)
  local copies, waits for them, and re-layouts  16.2 us (20%)
  matrix products  14.9 us (18%)
  starting transfers between devices  9.65 us (12%)
  waiting for transfers between devices  3.93 us (5%)
  other arithmetic  2.15 us (3%)
    dot_general x10, matrix products, per_block(): jnp.einsum('rd,bpd->brp', query_rows, block, preferred_element_type=jnp.f...  14.9 us
    all_gather x1, blocking collectives, body(): shard_rows = lax.all_gather(local_tokens, 'pages', axis=0, tiled=True)  13.7 us
    scatter x1, local copies, waits for them, and re-layouts, slot_plan(): codes = jnp.full((owner_count, CAP), -1, jnp.int32).at[holder, rank].set(...  10.2 us
    all_to_all x1, blocking collectives, body(): lax.all_to_all(picked, 'pages', split_axis=0, concat_axis=0, tiled=True)  9.92 us
    all_to_all x1, starting transfers between devices, body(): lax.all_to_all(codes, 'pages', split_axis=0, concat_axis=0, tiled=True)  6.35 us
    all_gather x1, blocking collectives, body(): local_tokens = lax.all_gather(queries, 'patches', axis=1, tiled=True)  5.37 us
    all_gather x1, blocking collectives, body(): page_scores = lax.all_gather(share_scores, 'patches', axis=0, tiled=True)  5.19 us
    all_to_all x1, waiting for transfers between devices, body(): lax.all_to_all(maxima, 'patches', split_axis=0, concat_axis=0, tiled=True)  3.93 us
  transfers between devices with their start and end apart: 2, of which 1 were waited for; matrix products, arithmetic and copies ran while one was open for 19% of the time, Pallas kernels for 0%

commit v1 on v0

v1 whole, which is shorter than its diff:
```python
import functools

import jax
import jax.numpy as jnp
from jax import lax
from jax.experimental import pallas as pl
from jax.experimental.pallas import tpu as pltpu
from jax.sharding import PartitionSpec as P

MESH = pl.DeviceIdType.MESH


def up(n, m):
    return -(-n // m) * m


def group_of(n, most):
    return max(d for d in range(1, most + 1) if n % d == 0)


def repeat(n, body):
    if n <= 16:
        for k in range(n):
            body(k)
    else:

        @pl.loop(0, n)
        def _(k):
            body(k)


def to_column(row):
    n = row.shape[1]
    eye = lax.broadcasted_iota(jnp.int32, (n, n), 0) == lax.broadcasted_iota(jnp.int32, (n, n), 1)
    return jnp.sum(jnp.where(eye, row, 0.0), axis=1, keepdims=True)


def to_row(column):
    n = column.shape[0]
    eye = lax.broadcasted_iota(jnp.int32, (n, n), 0) == lax.broadcasted_iota(jnp.int32, (n, n), 1)
    return jnp.sum(jnp.where(eye, column, 0.0), axis=0, keepdims=True)


def kernel(
    dims,
    q_ref,
    g_ref,
    rows_ref,
    cand_ref,
    out_ref,
    q_all,
    g_buf,
    best,
    best_in,
    send,
    arrived,
    g_sem,
    q_out,
    q_in,
    b_out,
    b_in,
    s_out,
    s_in,
):
    n_pages, n_patches, nq, tokens = dims
    devices = n_pages * n_patches
    page_count = g_ref.shape[0]
    share = page_count // n_patches
    me_g = lax.axis_index("groups")
    me_p = lax.axis_index("pages")
    me_j = lax.axis_index("patches")
    me = me_p * n_patches + me_j

    def owner(step):
        half = n_patches // 2
        chip, core = me_j // 2, lax.rem(me_j, 2)
        far = n_patches - 1 - step
        return lax.rem(chip + far // 2, half) * 2 + lax.rem(core + far, 2)

    def gallery_copy(step):
        first = owner(step) * share
        return pltpu.make_async_copy(
            g_ref.at[pl.ds(first, share)], g_buf.at[pl.ds(first, share)], g_sem.at[step]
        )

    for step in range(n_patches):
        gallery_copy(step).start()

    def peer(k):
        far = devices - 1 - k
        p = lax.rem(me_p + far // n_patches, n_pages)
        j = lax.rem(me_j + far % n_patches, n_patches)
        return p, j

    barrier = pltpu.get_barrier_semaphore()

    def greet(k):
        p, j = peer(k)
        pl.semaphore_signal(barrier, inc=1, device_id=(me_g, p, j), device_id_type=MESH)

    repeat(devices - 1, greet)

    q_all[me] = q_ref[...]
    send[...] = jnp.zeros_like(send)
    if best.shape[1] > share:
        best[:, share:, :] = jnp.zeros((best.shape[0], best.shape[1] - share, best.shape[2]), jnp.float32)
    page_rows = rows_ref[...].astype(jnp.float32)
    columns = []
    for q in range(nq):
        wanted = to_column(cand_ref[q : q + 1, :].astype(jnp.float32))
        ids = lax.broadcasted_iota(jnp.int32, (wanted.shape[0], page_rows.shape[1]), 1)
        hit = ids.astype(jnp.float32) == wanted
        columns.append(jnp.sum(jnp.where(hit, page_rows, 0.0), axis=1, keepdims=True))

    pl.semaphore_wait(barrier, devices - 1)

    def send_queries(k):
        p, j = peer(k)
        pltpu.make_async_remote_copy(
            src_ref=q_ref,
            dst_ref=q_all.at[me],
            send_sem=q_out,
            recv_sem=q_in,
            device_id=(me_g, p, j),
            device_id_type=MESH,
        ).start()

    repeat(devices - 1, send_queries)
    rest_q = q_all.at[pl.ds(0, devices - 1)]
    pltpu.make_async_copy(rest_q, rest_q, q_in).wait()

    unit = group_of(share, 5)
    token_rows = q_all[...].reshape(q_all.shape[0] * q_all.shape[1], q_all.shape[2])

    def best_copy(step):
        part = owner(step)
        return pltpu.make_async_remote_copy(
            src_ref=best.at[part],
            dst_ref=best_in.at[step],
            send_sem=b_out.at[step],
            recv_sem=b_in.at[step],
            device_id=(me_g, me_p, part),
            device_id_type=MESH,
        )

    for step in range(n_patches):
        part = owner(step)
        gallery_copy(step).wait()

        @pl.loop(0, share // unit)
        def _(block):
            for k in range(unit):
                page = block * unit + k
                sims = lax.dot_general(
                    g_buf[part * share + page],
                    token_rows,
                    (((1,), (1,)), ((), ())),
                    preferred_element_type=jnp.float32,
                )
                best[part, pl.ds(page, 1), :] = jnp.max(sims, axis=0, keepdims=True)

        if step < n_patches - 1:
            best_copy(step).start()

    width = best.shape[2]
    own_tokens = tokens // n_patches
    column = lax.broadcasted_iota(jnp.int32, (nq * n_pages, width), 1)
    query = lax.broadcasted_iota(jnp.int32, (nq * n_pages, width), 0)
    position = column // own_tokens
    named = position // (n_patches * nq) * nq + position % nq
    weights = jnp.where(named == query, 1.0 / tokens, 0.0)

    total = best[me_j]
    for step in range(n_patches - 1):
        best_copy(step).wait_recv()
        total = jnp.maximum(total, best_in[step])
    scores = lax.dot_general(
        weights,
        total,
        (((1,), (1,)), ((), ())),
        precision=lax.Precision.HIGHEST,
        preferred_element_type=jnp.float32,
    )
    for p in range(n_pages):
        send[p, :, : scores.shape[1]] = scores[p * nq : (p + 1) * nq, :]
    arrived[me] = send[me_p]

    def send_scores(k):
        p, j = peer(k)
        pltpu.make_async_remote_copy(
            src_ref=send.at[p],
            dst_ref=arrived.at[me],
            send_sem=s_out,
            recv_sem=s_in,
            device_id=(me_g, p, j),
            device_id_type=MESH,
        ).start()

    repeat(devices - 1, send_scores)
    rest_s = arrived.at[pl.ds(0, devices - 1)]
    pltpu.make_async_copy(rest_s, rest_s, s_in).wait()

    lanes = arrived.shape[2]
    spots = lax.broadcasted_iota(jnp.int32, (cand_ref.shape[1], lanes), 1).astype(jnp.float32)
    for q in range(nq):
        offset = columns[q] - spots

        def add(s, picked):
            first = jnp.float32(s * share) if isinstance(s, int) else (s * share).astype(jnp.float32)
            return picked + jnp.where(offset == first, arrived[s, q : q + 1, :], 0.0)

        picked = jnp.zeros(offset.shape, jnp.float32)
        if devices <= 16:
            for s in range(devices):
                picked = add(s, picked)
        else:
            picked = lax.fori_loop(0, devices, add, picked)
        out_ref[q : q + 1, :] = to_row(jnp.sum(picked, axis=1, keepdims=True))

    pltpu.make_async_copy(rest_q, rest_q, q_out).wait()
    for step in range(n_patches - 1):
        best_copy(step).wait_send()
    pltpu.make_async_copy(rest_s, rest_s, s_out).wait()


def body(queries, gallery, page_rows, candidates):
    nq, own_tokens, dim = queries.shape
    page_count, patches, _ = gallery.shape
    n_pages, n_patches = lax.axis_size("pages"), lax.axis_size("patches")
    devices = n_pages * n_patches
    share = page_count // n_patches
    rows = up(share, 8)
    width = devices * nq * own_tokens
    vmem = pl.BlockSpec(memory_space=pltpu.VMEM)
    dma = pltpu.SemaphoreType.DMA
    return pl.pallas_call(
        functools.partial(kernel, (n_pages, n_patches, nq, own_tokens * n_patches)),
        out_shape=jax.ShapeDtypeStruct(candidates.shape, jnp.float32),
        in_specs=[vmem, pl.BlockSpec(memory_space=pl.ANY), vmem, vmem],
        out_specs=vmem,
        scratch_shapes=[
            pltpu.VMEM((devices, nq * own_tokens, dim), jnp.bfloat16),
            pltpu.VMEM(gallery.shape, jnp.bfloat16),
            pltpu.VMEM((n_patches, rows, width), jnp.float32),
            pltpu.VMEM((n_patches, rows, width), jnp.float32),
            pltpu.VMEM((n_pages, nq, up(rows, 128)), jnp.float32),
            pltpu.VMEM((devices, nq, up(rows, 128)), jnp.float32),
            dma((n_patches,)),
            dma,
            dma,
            dma((n_patches,)),
            dma((n_patches,)),
            dma,
            dma,
        ],
        compiler_params=pltpu.CompilerParams(collective_id=0, has_side_effects=True),
    )(
        queries.reshape(nq * own_tokens, dim),
        gallery,
        page_rows.reshape(1, -1),
        candidates,
    )


def solution(mesh):
    in_specs = (
        P(("groups", "pages"), "patches", None),
        P(("groups", "pages"), "patches", None),
        P("groups"),
        P(("groups", "pages"), None),
    )
    out_specs = P(("groups", "pages"), None)
    return jax.shard_map(body, mesh=mesh, in_specs=in_specs, out_specs=out_specs, check_vma=False)
```

time: 82.3 us -> 24 us (0.29)
  blocking collectives: 34.2 us -> 0 us
  Pallas kernels: 0 us -> 21.3 us
  matrix products: 14.9 us -> 0 us
  local copies, waits for them, and re-layouts: 16.2 us -> 2.5 us
  starting transfers between devices: 9.65 us -> 0 us
  waiting for transfers between devices: 3.93 us -> 0 us
  other arithmetic: 2.15 us -> 0 us
    all_gather x3 -> x0, blocking collectives: 24.2 us -> none  [the longest x1 13.7 us: body(): shard_rows = lax.all_gather(local_tokens, 'pages', axis=0, tiled=True)]
    pallas_call x0 -> x1, Pallas kernels: none -> 21.3 us  [body(): pl.pallas_call(functools.partial(kernel, (n_pages, n_patches, nq, own_tok...]
    dot_general x10 -> x0, matrix products: 14.9 us -> none  [per_block(): jnp.einsum('rd,bpd->brp', query_rows, block, preferred_element_type=jnp.f...]
    scatter x1 -> x0, local copies, waits for them, and re-layouts: 10.2 us -> none  [slot_plan(): codes = jnp.full((owner_count, CAP), -1, jnp.int32).at[holder, rank].set(...]
    all_to_all x1 -> x0, blocking collectives: 9.92 us -> none  [body(): lax.all_to_all(picked, 'pages', split_axis=0, concat_axis=0, tiled=True)]
    all_to_all x2 -> x0, starting transfers between devices: 9.65 us -> none  [the longest x1 6.35 us: body(): lax.all_to_all(codes, 'pages', split_axis=0, concat_axis=0, tiled=True)]
    all_to_all x2 -> x0, waiting for transfers between devices: 3.93 us -> none  [the longest x1 3.93 us: body(): lax.all_to_all(maxima, 'patches', split_axis=0, concat_axis=0, tiled=True)]
    gather x5 -> x0, local copies, waits for them, and re-layouts: 3.01 us -> none  [the longest x2 1.26 us: body(): picked = page_scores[safe_codes % page_count, safe_codes // page_count]]
  transfers between devices with their start and end apart: 2 -> 0, of which waited for: 1 -> 0; matrix products, arithmetic and copies ran while one was open for 19% -> 0% of each run, Pallas kernels for 0% -> 0%
where the time goes in v1:
time: 24 us; the launch traced here: 23.8 us
  Pallas kernels  21.3 us (89%)
  local copies, waits for them, and re-layouts  2.5 us (10%)
    pallas_call x1, Pallas kernels, body(): pl.pallas_call(functools.partial(kernel, (n_pages, n_patches, nq, own_tok...  21.3 us
    reshape x1, local copies, waits for them, and re-layouts, body(): page_rows.reshape(1, -1)  1.27 us
    unnamed x1, local copies, waits for them, and re-layouts  1.22 us

profile of v1, /device:TPU:0, one launch (start us, length us, event | category | flops | bytes accessed | tf_op | source)
XLA Modules:
  0.0 23.8 jit_solution(5640520688747480699)
XLA Ops:
  0.0 1.3 %reshape.7.rows_ref = s32[1,320]{1,0:T(1,128)} reshape(s32[320]{0:T(512)} %param.6) | data formatting | bytes 2560 | tf_op jit(solution)/shard_map/reshape | solution.py:260
  1.3 21.3 %shard_map.46 = f32[2,32]{1,0:T(2,128)} custom-call(bf16[16,128]{1,0:T(8,128)(2,1)} %bitcast.1, bf16[80,256,128]{2,1,0:T(8,128)(2,1)} %g_ref.1, s32[1,320]{1,0:T(1,128)} %reshape.7.rows_ref, s32[2,32]{1,0:T(2,128)} %cand_ref.1), custom_call_target="tpu_custom_call" | custom-call | tf_op jit(solution)/shard_map/pallas_call | solution.py:236
  22.5 1.2 %copy.6 = f32[2,32]{1,0:T(2,128)} copy(f32[2,32]{1,0:T(2,128)} %shard_map.46) | data formatting | bytes 512

commit v2 on v1

--- a/solution.py
+++ b/solution.py
@@ -43,11 +43,14 @@
 
 def kernel(
     dims,
+    q_hbm,
+    g_ref,
+    rows_hbm,
+    cand_hbm,
+    out_ref,
     q_ref,
-    g_ref,
     rows_ref,
     cand_ref,
-    out_ref,
     q_all,
     g_buf,
     best,
@@ -55,6 +58,7 @@
     send,
     arrived,
     g_sem,
+    a_sem,
     q_out,
     q_in,
     b_out,
@@ -83,9 +87,6 @@
             g_ref.at[pl.ds(first, share)], g_buf.at[pl.ds(first, share)], g_sem.at[step]
         )
 
-    for step in range(n_patches):
-        gallery_copy(step).start()
-
     def peer(k):
         far = devices - 1 - k
         p = lax.rem(me_p + far // n_patches, n_pages)
@@ -99,12 +100,24 @@
         pl.semaphore_signal(barrier, inc=1, device_id=(me_g, p, j), device_id_type=MESH)
 
     repeat(devices - 1, greet)
-
-    q_all[me] = q_ref[...]
+    small = [
+        pltpu.make_async_copy(source, target, a_sem.at[k])
+        for k, (source, target) in enumerate(
+            ((q_hbm, q_ref), (cand_hbm, cand_ref), (rows_hbm, rows_ref))
+        )
+    ]
+    for copy in small:
+        copy.start()
+    for step in range(n_patches):
+        gallery_copy(step).start()
     send[...] = jnp.zeros_like(send)
     if best.shape[1] > share:
         best[:, share:, :] = jnp.zeros((best.shape[0], best.shape[1] - share, best.shape[2]), jnp.float32)
-    page_rows = rows_ref[...].astype(jnp.float32)
+    for copy in small:
+        copy.wait()
+
+    q_all[me] = q_ref[...]
+    page_rows = rows_ref[...].astype(jnp.float32).reshape(1, -1)
     columns = []
     for q in range(nq):
         wanted = to_column(cand_ref[q : q + 1, :].astype(jnp.float32))
@@ -129,7 +142,7 @@
     rest_q = q_all.at[pl.ds(0, devices - 1)]
     pltpu.make_async_copy(rest_q, rest_q, q_in).wait()
 
-    unit = group_of(share, 5)
+    unit = group_of(share, 20)
     token_rows = q_all[...].reshape(q_all.shape[0] * q_all.shape[1], q_all.shape[2])
 
     def best_copy(step):
@@ -147,10 +160,9 @@
         part = owner(step)
         gallery_copy(step).wait()
 
-        @pl.loop(0, share // unit)
-        def _(block):
+        def block(start):
             for k in range(unit):
-                page = block * unit + k
+                page = start + k
                 sims = lax.dot_general(
                     g_buf[part * share + page],
                     token_rows,
@@ -158,6 +170,11 @@
                     preferred_element_type=jnp.float32,
                 )
                 best[part, pl.ds(page, 1), :] = jnp.max(sims, axis=0, keepdims=True)
+
+        if unit == share:
+            block(0)
+        else:
+            pl.loop(0, share, step=unit)(block)
 
         if step < n_patches - 1:
             best_copy(step).start()
@@ -235,10 +252,13 @@
     dma = pltpu.SemaphoreType.DMA
     return pl.pallas_call(
         functools.partial(kernel, (n_pages, n_patches, nq, own_tokens * n_patches)),
-        out_shape=jax.ShapeDtypeStruct(candidates.shape, jnp.float32),
-        in_specs=[vmem, pl.BlockSpec(memory_space=pl.ANY), vmem, vmem],
+        out_shape=pltpu.VMEM(candidates.shape, jnp.float32),
+        in_specs=[pl.BlockSpec(memory_space=pl.ANY)] * 4,
         out_specs=vmem,
         scratch_shapes=[
+            pltpu.VMEM((nq * own_tokens, dim), jnp.bfloat16),
+            pltpu.VMEM(page_rows.shape, jnp.int32),
+            pltpu.VMEM(candidates.shape, jnp.int32),
             pltpu.VMEM((devices, nq * own_tokens, dim), jnp.bfloat16),
             pltpu.VMEM(gallery.shape, jnp.bfloat16),
             pltpu.VMEM((n_patches, rows, width), jnp.float32),
@@ -246,6 +266,7 @@
             pltpu.VMEM((n_pages, nq, up(rows, 128)), jnp.float32),
             pltpu.VMEM((devices, nq, up(rows, 128)), jnp.float32),
             dma((n_patches,)),
+            dma((3,)),
             dma,
             dma,
             dma((n_patches,)),
@@ -257,7 +278,7 @@
     )(
         queries.reshape(nq * own_tokens, dim),
         gallery,
-        page_rows.reshape(1, -1),
+        page_rows,
         candidates,
     )
 

time: 24 us -> 19.3 us (0.80)
  Pallas kernels: 21.3 us -> 18.6 us
  local copies, waits for them, and re-layouts: 2.5 us -> 0.56 us
    pallas_call x1, Pallas kernels: 21.3 us -> 18.6 us  [body(): pl.pallas_call(functools.partial(kernel, (n_pages, n_patches, nq, own_tok...]
    reshape x1 -> x0, local copies, waits for them, and re-layouts: 1.27 us -> none  [body(): page_rows.reshape(1, -1)]
    unnamed x1, local copies, waits for them, and re-layouts: 1.22 us -> 0.56 us
where the time goes in v2:
time: 19.3 us; the launch traced here: 19.2 us
  Pallas kernels  18.6 us (96%)
  local copies, waits for them, and re-layouts  0.56 us (3%)
    pallas_call x1, Pallas kernels, body(): pl.pallas_call(functools.partial(kernel, (n_pages, n_patches, nq, own_tok...  18.6 us
    unnamed x1, local copies, waits for them, and re-layouts  0.56 us

profile of v2, /device:TPU:0, one launch (start us, length us, event | category | flops | bytes accessed | tf_op | source)
XLA Modules:
  0.0 19.2 jit_solution(7356246952113533791)
XLA Ops:
  0.0 18.6 %shard_map.46 = f32[2,32]{1,0:T(2,128)S(1)} custom-call(bf16[16,128]{1,0:T(8,128)(2,1)} %bitcast.1, bf16[80,256,128]{2,1,0:T(8,128)(2,1)} %g_ref.1, s32[320]{0:T(512)} %rows_hbm.1, s32[2,32]{1,0:T(2,128)} %cand_hbm.1), custom_call_target="tpu_custom_call" | custom-call | tf_op jit(solution)/shard_map/pallas_call | solution.py:253
  18.6 0.6 %copy.6 = f32[2,32]{1,0:T(2,128)} copy(f32[2,32]{1,0:T(2,128)S(1)} %shard_map.46) | data formatting | bytes 512

commit v3 on v2

--- a/solution.py
+++ b/solution.py
@@ -39,6 +39,15 @@
     n = column.shape[0]
     eye = lax.broadcasted_iota(jnp.int32, (n, n), 0) == lax.broadcasted_iota(jnp.int32, (n, n), 1)
     return jnp.sum(jnp.where(eye, column, 0.0), axis=0, keepdims=True)
+
+
+def top_row(sims):
+    rows, width = sims.shape
+    chains = 4
+    if rows % (8 * chains) == 0:
+        sims = jnp.max(sims.reshape(rows // (8 * chains), chains, 8, width), axis=0)
+        sims = jnp.maximum(jnp.maximum(sims[0], sims[1]), jnp.maximum(sims[2], sims[3]))
+    return jnp.max(sims, axis=0, keepdims=True)
 
 
 def kernel(
@@ -111,8 +120,9 @@
     for step in range(n_patches):
         gallery_copy(step).start()
     send[...] = jnp.zeros_like(send)
-    if best.shape[1] > share:
-        best[:, share:, :] = jnp.zeros((best.shape[0], best.shape[1] - share, best.shape[2]), jnp.float32)
+    if best.shape[2] > share:
+        spare = best.at[:, :, share:, :]
+        spare[...] = jnp.zeros(spare.shape, jnp.float32)
     for copy in small:
         copy.wait()
 
@@ -127,23 +137,55 @@
 
     pl.semaphore_wait(barrier, devices - 1)
 
+    half_pages = n_pages // 2
+    half_devices = devices // 2
+    my_half = me_p // half_pages
+
     def send_queries(k):
         p, j = peer(k)
         pltpu.make_async_remote_copy(
             src_ref=q_ref,
             dst_ref=q_all.at[me],
             send_sem=q_out,
-            recv_sem=q_in,
+            recv_sem=q_in.at[lax.rem(p // half_pages + my_half, 2)],
             device_id=(me_g, p, j),
             device_id_type=MESH,
         ).start()
 
     repeat(devices - 1, send_queries)
     rest_q = q_all.at[pl.ds(0, devices - 1)]
-    pltpu.make_async_copy(rest_q, rest_q, q_in).wait()
 
     unit = group_of(share, 20)
-    token_rows = q_all[...].reshape(q_all.shape[0] * q_all.shape[1], q_all.shape[2])
+
+    def half_weights(half, others):
+        some = q_all.at[pl.ds(0, others)]
+        pltpu.make_async_copy(some, some, q_in.at[0 if others < half_devices else 1]).wait()
+        rows = q_all[pl.ds(half * half_devices, half_devices)]
+        rows = rows.reshape(rows.shape[0] * rows.shape[1], rows.shape[2])
+        none = jnp.zeros_like(rows)
+        return jnp.concatenate(
+            [jnp.concatenate([rows, none], axis=1), jnp.concatenate([none, rows], axis=1)], axis=0
+        )
+
+    def part_maxima(part, half, weights):
+        def block(start):
+            for k in range(0, unit, 2):
+                first, second = start + k, start + min(k + 1, unit - 1)
+                pair = jnp.concatenate(
+                    [g_buf[part * share + first], g_buf[part * share + second]], axis=1
+                )
+                sims = lax.dot_general(
+                    pair, weights, (((1,), (1,)), ((), ())), preferred_element_type=jnp.float32
+                )
+                row = top_row(sims)
+                width = row.shape[1] // 2
+                best[part, half, pl.ds(first, 1), :] = row[:, :width]
+                best[part, half, pl.ds(second, 1), :] = row[:, width:]
+
+        if unit == share:
+            block(0)
+        else:
+            pl.loop(0, share, step=unit)(block)
 
     def best_copy(step):
         part = owner(step)
@@ -156,30 +198,17 @@
             device_id_type=MESH,
         )
 
+    weights = half_weights(my_half, half_devices - 1)
     for step in range(n_patches):
-        part = owner(step)
         gallery_copy(step).wait()
-
-        def block(start):
-            for k in range(unit):
-                page = start + k
-                sims = lax.dot_general(
-                    g_buf[part * share + page],
-                    token_rows,
-                    (((1,), (1,)), ((), ())),
-                    preferred_element_type=jnp.float32,
-                )
-                best[part, pl.ds(page, 1), :] = jnp.max(sims, axis=0, keepdims=True)
-
-        if unit == share:
-            block(0)
-        else:
-            pl.loop(0, share, step=unit)(block)
-
+        part_maxima(owner(step), my_half, weights)
+    weights = half_weights(1 - my_half, half_devices)
+    for step in range(n_patches):
+        part_maxima(owner(step), 1 - my_half, weights)
         if step < n_patches - 1:
             best_copy(step).start()
 
-    width = best.shape[2]
+    width = 2 * best.shape[3]
     own_tokens = tokens // n_patches
     column = lax.broadcasted_iota(jnp.int32, (nq * n_pages, width), 1)
     query = lax.broadcasted_iota(jnp.int32, (nq * n_pages, width), 0)
@@ -191,12 +220,15 @@
     for step in range(n_patches - 1):
         best_copy(step).wait_recv()
         total = jnp.maximum(total, best_in[step])
-    scores = lax.dot_general(
-        weights,
-        total,
-        (((1,), (1,)), ((), ())),
-        precision=lax.Precision.HIGHEST,
-        preferred_element_type=jnp.float32,
+    scores = sum(
+        lax.dot_general(
+            weights[:, half * best.shape[3] : (half + 1) * best.shape[3]],
+            total[half],
+            (((1,), (1,)), ((), ())),
+            precision=lax.Precision.HIGHEST,
+            preferred_element_type=jnp.float32,
+        )
+        for half in range(2)
     )
     for p in range(n_pages):
         send[p, :, : scores.shape[1]] = scores[p * nq : (p + 1) * nq, :]
@@ -261,14 +293,14 @@
             pltpu.VMEM(candidates.shape, jnp.int32),
             pltpu.VMEM((devices, nq * own_tokens, dim), jnp.bfloat16),
             pltpu.VMEM(gallery.shape, jnp.bfloat16),
-            pltpu.VMEM((n_patches, rows, width), jnp.float32),
-            pltpu.VMEM((n_patches, rows, width), jnp.float32),
+            pltpu.VMEM((n_patches, 2, rows, width // 2), jnp.float32),
+            pltpu.VMEM((n_patches, 2, rows, width // 2), jnp.float32),
             pltpu.VMEM((n_pages, nq, up(rows, 128)), jnp.float32),
             pltpu.VMEM((devices, nq, up(rows, 128)), jnp.float32),
             dma((n_patches,)),
             dma((3,)),
             dma,
-            dma,
+            dma((2,)),
             dma((n_patches,)),
             dma((n_patches,)),
             dma,

time: 19.3 us -> 19.7 us (1.021)
  Pallas kernels: 18.6 us -> 19 us
    pallas_call x1, Pallas kernels: 18.6 us -> 19 us  [body(): pl.pallas_call(functools.partial(kernel, (n_pages, n_patches, nq, own_tok...]
where the time goes in v3:
time: 19.7 us; the launch traced here: 19.6 us
  Pallas kernels  19 us (96%)
  local copies, waits for them, and re-layouts  0.56 us (3%)
    pallas_call x1, Pallas kernels, body(): pl.pallas_call(functools.partial(kernel, (n_pages, n_patches, nq, own_tok...  19 us
    unnamed x1, local copies, waits for them, and re-layouts  0.56 us

profile of v3, /device:TPU:0, one launch (start us, length us, event | category | flops | bytes accessed | tf_op | source)
XLA Modules:
  0.0 19.6 jit_solution(3902084522331571023)
XLA Ops:
  0.0 19.0 %shard_map.46 = f32[2,32]{1,0:T(2,128)S(1)} custom-call(bf16[16,128]{1,0:T(8,128)(2,1)} %bitcast.1, bf16[80,256,128]{2,1,0:T(8,128)(2,1)} %g_ref.1, s32[320]{0:T(512)} %rows_hbm.1, s32[2,32]{1,0:T(2,128)} %cand_hbm.1), custom_call_target="tpu_custom_call" | custom-call | tf_op jit(solution)/shard_map/pallas_call | solution.py:285
  19.0 0.6 %copy.6 = f32[2,32]{1,0:T(2,128)} copy(f32[2,32]{1,0:T(2,128)S(1)} %shard_map.46) | data formatting | bytes 512

commit v4 on v3

--- a/solution.py
+++ b/solution.py
@@ -198,9 +198,10 @@
             device_id_type=MESH,
         )
 
+    for step in range(n_patches):
+        gallery_copy(step).wait()
     weights = half_weights(my_half, half_devices - 1)
     for step in range(n_patches):
-        gallery_copy(step).wait()
         part_maxima(owner(step), my_half, weights)
     weights = half_weights(1 - my_half, half_devices)
     for step in range(n_patches):

time: 19.7 us -> 19.1 us (0.970)
  Pallas kernels: 19 us -> 18.4 us
    pallas_call x1, Pallas kernels: 19 us -> 18.4 us  [body(): pl.pallas_call(functools.partial(kernel, (n_pages, n_patches, nq, own_tok...]
where the time goes in v4:
time: 19.1 us; the launch traced here: 18.9 us
  Pallas kernels  18.4 us (96%)
  local copies, waits for them, and re-layouts  0.56 us (3%)
    pallas_call x1, Pallas kernels, body(): pl.pallas_call(functools.partial(kernel, (n_pages, n_patches, nq, own_tok...  18.4 us
    unnamed x1, local copies, waits for them, and re-layouts  0.56 us

profile of v4, /device:TPU:0, one launch (start us, length us, event | category | flops | bytes accessed | tf_op | source)
XLA Modules:
  0.0 18.9 jit_solution(11482510503954362007)
XLA Ops:
  0.0 18.4 %shard_map.46 = f32[2,32]{1,0:T(2,128)S(1)} custom-call(bf16[16,128]{1,0:T(8,128)(2,1)} %bitcast.1, bf16[80,256,128]{2,1,0:T(8,128)(2,1)} %g_ref.1, s32[320]{0:T(512)} %rows_hbm.1, s32[2,32]{1,0:T(2,128)} %cand_hbm.1), custom_call_target="tpu_custom_call" | custom-call | tf_op jit(solution)/shard_map/pallas_call | solution.py:286
  18.4 0.6 %copy.6 = f32[2,32]{1,0:T(2,128)} copy(f32[2,32]{1,0:T(2,128)S(1)} %shard_map.46) | data formatting | bytes 512
